TPU v7x, 32 devices: a whole 2x2x4 slice. The times are simulated.
32 devices in a mesh: ctx: 2 (over core), head: 4 (over y, x), doc: 4 (over z).
Axes of the slice: x: 2, y: 2, z: 4, core: 2. Of those that a mesh axis runs over, the one named last changes fastest.
Arguments:
- queries: bfloat16 [4, 256, 8192], P('doc', 'ctx', 'head'), may hold values from -360 to 360
- keys: bfloat16 [4, 8192, 1024], P('doc', 'ctx', 'head'), may hold values from -6 to 6
- values: bfloat16 [4, 8192, 1024], P('doc', 'ctx', 'head'), may hold values from -6 to 6
- pattern: int32 [4, 2, 16], P('doc'), may hold values from 0 to 63, as said below
Outputs:
- attended: bfloat16 [4, 256, 8192], P('doc', 'ctx', 'head')
- gram: float32 [8192, 8192], P(('head', 'ctx'), 'doc')
Inputs may be any that keep to these rules, and one draw needn't show every extreme that they name: Each row pattern[d, b, :] lists 16 different block numbers; no context shard (blocks s * 32 to (s + 1) * 32 - 1) holds more than 12 of one row's blocks, and in every draw some row has exactly 12 of its blocks in one shard.
All inputs are finite; a program needn't handle non-finite values.
Results may differ from a plain program's by a relative error of at most 0.015.
Values may be sent and summed in bfloat16 or wider, within the bound.
A program may use at most 128 MiB of HBM per device.

v0:
```python
import functools
import math

import jax
import jax.numpy as jnp
from jax import lax
from jax.experimental import pallas as pl
from jax.experimental.pallas import tpu as pltpu
from jax.sharding import PartitionSpec as P

HEAD_SIZE = 128
BLOCK_TOKENS = 128
GROUP = 8
WIDE = 2 * HEAD_SIZE
LAG = 4
MESH = pl.DeviceIdType.MESH


def pack_kernel(pat, k_ref, v_ref, own_ref, give_ref, sem):
    c = lax.axis_index("ctx")
    entries = pat.shape[2]
    shard_blocks = k_ref.shape[0] // BLOCK_TOKENS

    def each(action, otherwise):
        for n, (row, out_ref) in enumerate(((1 - c, give_ref), (c, own_ref))):
            for p in range(entries):
                at = pat[0, row, p] - c * shard_blocks
                mine = jnp.logical_and(at >= 0, at < shard_blocks)
                here = pl.ds(p * BLOCK_TOKENS, BLOCK_TOKENS)

                @pl.when(mine)
                def _():
                    there = pl.ds(pl.multiple_of(at * BLOCK_TOKENS, BLOCK_TOKENS), BLOCK_TOKENS)
                    for m, ref in enumerate((k_ref, v_ref)):
                        action(pltpu.make_async_copy(ref.at[there, :], out_ref.at[m, here, :], sem.at[n, m, p]))

                if otherwise:
                    @pl.when(jnp.logical_not(mine))
                    def _():
                        zero = jnp.zeros((BLOCK_TOKENS, k_ref.shape[1]), out_ref.dtype)
                        out_ref[0, here, :] = zero
                        out_ref[1, here, :] = zero

    each(lambda copy: copy.start(), True)
    each(lambda copy: copy.wait(), False)


def main_kernel(docs, gather, q_any, own_any, give_any, att_ref, *refs):
    if gather:
        (rows_ref, cols_ref, q_ref, own, recv, kv, in_sem, kv_send, kv_recv, gath, colbuf,
         z_up, z_down, z_recv, x_send, x_more, x_recv, r_send, r_recv, p_send, p_recv, r_local, c_local) = refs
    else:
        q_ref, own, recv, kv, in_sem, kv_send, kv_recv = refs
    c = lax.axis_index("ctx")
    h = lax.axis_index("head")
    d = lax.axis_index("doc")
    peer = 1 - c
    tokens, width = q_ref.shape
    chunks = width // WIDE
    x_next = h + 1 - 2 * (h % 2)
    y_next = (h + 2) % 4

    take_q = pltpu.make_async_copy(q_any, q_ref, in_sem.at[0])
    take_own = pltpu.make_async_copy(own_any, own, in_sem.at[1])
    take_own.start()
    take_q.start()

    barrier = pltpu.get_barrier_semaphore()

    def greet(where):
        pl.semaphore_signal(barrier, inc=1, device_id=where, device_id_type=MESH)

    greet({"ctx": peer})
    if gather:
        greet({"head": x_next})
        greet({"head": y_next})

        @pl.when(d > 0)
        def _():
            greet({"doc": d - 1})

        @pl.when(d < docs - 1)
        def _():
            greet({"doc": d + 1})

        ends = jnp.where(d > 0, 1, 0) + jnp.where(d < docs - 1, 1, 0)
        pl.semaphore_wait(barrier, 3 + ends)
    else:
        pl.semaphore_wait(barrier, 1)

    def remote(src, dst, send, arrive, where):
        return pltpu.make_async_remote_copy(src_ref=src, dst_ref=dst, send_sem=send, recv_sem=arrive,
                                            device_id=where, device_id_type=MESH)

    swaps = [remote(give_any.at[n], recv.at[n], kv_send.at[n], kv_recv.at[n], {"ctx": peer}) for n in range(2)]
    for swap in swaps:
        swap.start()
    take_q.wait()
    take_own.wait()
    for n, swap in enumerate(swaps):
        swap.wait()
        kv[n] = own[n] + recv[n]

    factor = HEAD_SIZE ** (-0.5) * math.log2(math.e)

    def two_heads(t):
        at = pl.multiple_of(t * WIDE, WIDE)
        pair = q_ref[:, pl.ds(at, WIDE)]
        q2 = jnp.concatenate([pair[:, :HEAD_SIZE], pair[:, HEAD_SIZE:]], axis=0)
        lane = pl.ds(pl.multiple_of((t * 2 // GROUP) * HEAD_SIZE, HEAD_SIZE), HEAD_SIZE)
        scores = lax.dot_general(q2, kv[0, :, lane], (((1,), (1,)), ((), ())),
                                 preferred_element_type=jnp.float32)
        top = jnp.max(scores, axis=-1, keepdims=True)
        weights = jnp.exp2((scores - top) * factor)
        total = jnp.sum(weights, axis=-1, keepdims=True)
        mixed = jnp.dot(weights.astype(jnp.bfloat16), kv[1, :, lane], preferred_element_type=jnp.float32)
        out = (mixed / total).astype(jnp.bfloat16)
        out = jnp.concatenate([out[:tokens], out[tokens:]], axis=1)
        if gather:
            gath[d, t] = out
        att_ref[:, pl.ds(at, WIDE)] = out

    if not gather:
        def plain(t, carry):
            two_heads(t)
            return carry

        lax.fori_loop(0, chunks, plain, 0)
        return

    total_events = docs * chunks
    far_step = docs // 2
    half_chunks = chunks // 2
    rx = (h % 2 + d % 2) % 2
    ry = (h // 2 + d // 2) % 2

    def columns(k):
        return pl.ds(pl.multiple_of(k * WIDE, WIDE), WIDE)

    def up(i, k):
        return remote(gath.at[i, k], gath.at[i, k], z_up.at[i, k], z_recv.at[i, k], {"doc": d + 1})

    def down(i, k):
        return remote(gath.at[i, k], gath.at[i, k], z_down.at[i, k], z_recv.at[i, k], {"doc": d - 1})

    def row_home(i, k):
        return rows_ref.at[i, c, :, columns(k % half_chunks)]

    def row_copy(i, k):
        return remote(gath.at[i, k], row_home(i, k), r_send.at[i, k], r_recv.at[i, k], {"ctx": peer})

    def row_local(i, k):
        return pltpu.make_async_copy(gath.at[i, k], row_home(i, k), r_local.at[i, k])

    def col_local(i, k, src):
        return pltpu.make_async_copy(src.at[i, k], cols_ref.at[i, c, :, columns(k)], c_local.at[i, k])

    def col_copy(i, k, src):
        return remote(src.at[i, k], cols_ref.at[i, c, :, columns(k)],
                      p_send.at[i, k], p_recv.at[i, k], {"ctx": peer})

    def plane_copy(i, k, src, sem, head):
        return remote(src.at[i, k], colbuf.at[i, k], sem.at[i, k], x_recv.at[i, k], {"head": head})

    def place(k):
        even = k % 2 == 0
        return (jnp.where(even, rx, ry), jnp.where(even, ry, rx),
                jnp.where(even, x_next, y_next), jnp.where(even, y_next, x_next))

    def item(side, s):
        i = d - s if side == 0 else d + s
        there = (i >= 0) if side == 0 else jnp.logical_and(i < docs, s > 0)
        return i, there

    def z_part(e):
        s, k = e // chunks, e % chunks
        for side in range(2):
            i, there = item(side, s)

            @pl.when(jnp.logical_and(there, e < total_events))
            def _():
                @pl.when(s > 0)
                def _():
                    up(i, k).wait_recv()

                @pl.when(jnp.logical_and(i <= d, d < docs - 1))
                def _():
                    up(i, k).start()

                @pl.when(jnp.logical_and(i >= d, d > 0))
                def _():
                    down(i, k).start()

                @pl.when(k // half_chunks == c)
                def _():
                    row_local(i, k).start()

                @pl.when(k // half_chunks != c)
                def _():
                    row_copy(i, k).start()

    def x_part(e):
        a, b, first, second = place(e)
        hop = a + b * (3 - 2 * a)
        ee = e - LAG * hop
        inside = jnp.logical_and(ee >= 0, ee < total_events)
        at = jnp.where(inside, ee, 0)
        s, k = at // chunks, at % chunks
        near = s < far_step
        for side in range(2):
            i, there = item(side, s)
            there = jnp.logical_and(there, inside)

            @pl.when(jnp.logical_and(there, hop == 0))
            def _():
                plane_copy(i, k, gath, x_send, first).start()

                @pl.when(s >= far_step)
                def _():
                    plane_copy(i, k, gath, x_more, second).start()

                col_copy(i, k, gath).start()
                col_local(i, k, gath).start()

            @pl.when(jnp.logical_and(there, hop > 0))
            def _():
                plane_copy(i, k, colbuf, x_send, first).wait_recv()

                @pl.when(hop == 1)
                def _():
                    plane_copy(i, k, colbuf, x_send, second).start()

                @pl.when(jnp.logical_and(hop == 2, near))
                def _():
                    plane_copy(i, k, colbuf, x_send, first).start()

                col_copy(i, k, colbuf).start()
                col_local(i, k, colbuf).start()

    def opening(e, carry):
        two_heads(e)
        z_part(e)
        x_part(e)
        return carry

    def event(e, carry):
        z_part(e)
        x_part(e)
        return carry

    lax.fori_loop(0, chunks, opening, 0)
    lax.fori_loop(chunks, total_events + 3 * LAG, event, 0)

    def finish(n, carry):
        i, k = n // chunks, n % chunks
        a, b, first, second = place(k)
        hop = a + b * (3 - 2 * a)
        near = jnp.logical_and(i - d < far_step, d - i < far_step)

        @pl.when(jnp.logical_and(i <= d, d < docs - 1))
        def _():
            up(i, k).wait_send()

        @pl.when(jnp.logical_and(i >= d, d > 0))
        def _():
            down(i, k).wait_send()

        @pl.when(k // half_chunks == c)
        def _():
            row_local(i, k).wait()
            row_copy(i, k).wait_recv()

        @pl.when(k // half_chunks != c)
        def _():
            row_copy(i, k).wait_send()

        col_copy(i, k, colbuf).wait()
        col_local(i, k, colbuf).wait()

        @pl.when(jnp.logical_or(hop < 2, jnp.logical_and(hop == 2, near)))
        def _():
            plane_copy(i, k, colbuf, x_send, first).wait_send()

        @pl.when(jnp.logical_and(hop == 0, jnp.logical_not(near)))
        def _():
            plane_copy(i, k, colbuf, x_more, second).wait_send()

        return carry

    lax.fori_loop(0, total_events, finish, 0)


def fused(queries, keys, values, pattern, docs, gather):
    tokens, width = queries.shape
    wide = keys.shape[1]
    entries = pattern.shape[2]
    bf16 = jnp.bfloat16
    vmem = pl.BlockSpec(memory_space=pltpu.VMEM)
    smem = pl.BlockSpec(memory_space=pltpu.SMEM)
    hbm = pl.BlockSpec(memory_space=pl.ANY)
    pack = (2, entries * BLOCK_TOKENS, wide)
    own, give = pl.pallas_call(
        pack_kernel,
        out_shape=[jax.ShapeDtypeStruct(pack, bf16)] * 2,
        in_specs=[smem, hbm, hbm],
        out_specs=[vmem] * 2,
        scratch_shapes=[pltpu.SemaphoreType.DMA((2, 2, entries))],
    )(pattern, keys, values)
    out_shape = [jax.ShapeDtypeStruct((tokens, width), bf16)]
    scratch = [pltpu.VMEM((tokens, width), bf16)] + [pltpu.VMEM(pack, bf16)] * 3
    scratch += [pltpu.SemaphoreType.DMA((2,))] * 3
    if gather:
        chunks = width // WIDE
        out_shape += [
            jax.ShapeDtypeStruct((docs, 2, tokens, width // 2), bf16),
            jax.ShapeDtypeStruct((docs, 2, tokens, width), bf16),
        ]
        scratch += [pltpu.VMEM((docs, chunks, tokens, WIDE), bf16)] * 2
        scratch += [pltpu.SemaphoreType.DMA((docs, chunks))] * 12
    return pl.pallas_call(
        functools.partial(main_kernel, docs, gather),
        out_shape=out_shape,
        in_specs=[hbm] * 3,
        out_specs=[vmem] + [hbm] * (len(out_shape) - 1),
        scratch_shapes=scratch,
        compiler_params=pltpu.CompilerParams(collective_id=0, has_side_effects=True),
    )(queries, own, give)


def per_device(queries, keys, values, pattern):
    ctx_count = lax.axis_size("ctx")
    head_count = lax.axis_size("head")
    doc_count = lax.axis_size("doc")
    owner = lax.axis_index("ctx")
    tok_rows = queries.shape[1]
    width = queries.shape[2]
    direct = head_count == 4 and doc_count == 4
    made = fused(queries[0], keys[0], values[0], pattern, doc_count, direct)
    contract = (((0,), (0,)), ((), ()))
    if direct:
        attended, rows, cols = made
        tokens = doc_count * ctx_count * tok_rows
        product = lax.dot_general(
            rows.reshape(tokens, width // ctx_count), cols.reshape(tokens, width), contract,
            preferred_element_type=jnp.float32)
        return (attended[None], product)
    attended = made[0]
    sub = width // ctx_count
    model_width = width * head_count
    span = lax.all_gather(attended, "ctx", axis=0, tiled=True)
    mine_cols = lax.dynamic_slice_in_dim(span, owner * sub, sub, 1)
    full_doc = lax.all_gather(span, "head", axis=1, tiled=True)
    slice_width = model_width // doc_count
    split_cols = full_doc.reshape(tok_rows * ctx_count, doc_count, slice_width)
    column_set = lax.all_to_all(split_cols, "doc", split_axis=1, concat_axis=0, tiled=True).reshape(
        doc_count * tok_rows * ctx_count, slice_width)
    product = lax.dot_general(
        lax.all_gather(mine_cols, "doc", axis=0, tiled=True), column_set, contract,
        preferred_element_type=jnp.float32)
    return (attended[None], product)


def solution(mesh):
    placed = (
        P("doc", "ctx", "head"),
        P("doc", "ctx", "head"),
        P("doc", "ctx", "head"),
        P("doc", None, None),
    )
    return jax.shard_map(
        per_device,
        mesh=mesh,
        in_specs=placed,
        out_specs=(P("doc", "ctx", "head"), P(("head", "ctx"), "doc")),
        check_vma=False,
    )
```

profile of v0, /device:TPU:25, one launch (start us, length us, event | category | flops | bytes accessed | tf_op | source)
XLA Modules:
  0.0 74.9 jit_solution(171699309801570781)
XLA Ops:
  0.6 4.7 %shard_map.59 = (bf16[2,2048,256]{2,1,0:T(8,128)(2,1)}, bf16[2,2048,256]{2,1,0:T(8,128)(2,1)}) custom-call(s32[1,2,16]{2,1,0:T(2,128)} %pat.1, bf16[4096,256]{1,0:T(8,128)(2,1)} %bitcast.10, bf16[4096,256]{1,0:T(8,128)(2,1)} %bitcast.11), custom_call_target="tpu_custom_call" | custom-call | tf_op jit(solution)/shard_map/pallas_call | solution.py:302
  5.3 58.0 %shard_map.60 = (bf16[128,2048]{1,0:T(8,128)(2,1)}, bf16[4,2,128,1024]{3,2,1,0:T(8,128)(2,1)}, bf16[4,2,128,2048]{3,2,1,0:T(8,128)(2,1)}) custom-call(bf16[128,2048]{1,0:T(8,128)(2,1)} %bitcast.12, bf16[2,2048,256]{2,1,0:T(8,128)(2,1)} %get-tuple-element.7.own_any, bf16[2,2048,256]{2,1,0:T(8,128)(2,1)} %get-tuple-element.8.give_any), custom_call_target="tpu_custom_call" | custom-call | tf_op jit(solution)/shard_map/pallas_call | solution.py:320
  63.3 0.0 copy-start
  63.3 10.8 %convolution_bitcast_fusion = f32[1024,2048]{1,0:T(8,128)} fusion(bf16[4,2,128,1024]{3,2,1,0:T(8,128)(2,1)} %get-tuple-element.10, bf16[4,2,128,2048]{3,2,1,0:T(8,128)(2,1)} %get-tuple-element.11), kind=kOutput, calls=%fused_computation | convolution fusion | flops 4294967296 | bytes 14680064 | tf_op jit(solution)/shard_map/dot_general | solution.py:343
  74.2 0.0 copy-done
  74.2 0.8 %copy.10 = bf16[1,128,2048]{2,1,0:T(8,128)(2,1)} copy(bf16[1,128,2048]{2,1,0:T(8,128)(2,1)S(1)} %bitcast.13) | data formatting | bytes 1048576
Async XLA Ops:
  63.3 10.9 %copy-start = (bf16[128,2048]{1,0:T(8,128)(2,1)S(1)}, bf16[128,2048]{1,0:T(8,128)(2,1)}, u32[]{:S(2)}) copy-start(bf16[128,2048]{1,0:T(8,128)(2,1)} %get-tuple-element.9) | copy-start | bytes 1572868
where the time goes:
time: 74.9 us
  Pallas kernels  62.7 us (84%)
  matrix products  10.8 us (14%)
  local copies, waits for them, and re-layouts  0.8 us (1%)
    pallas_call x1, Pallas kernels, fused(): pl.pallas_call(functools.partial(main_kernel, docs, gather), out_shape=ou...  58 us
    dot_general x1, matrix products, per_device(): lax.dot_general(rows.reshape(tokens, width // ctx_count), cols.reshape(to...  10.8 us
    pallas_call x1, Pallas kernels, fused(): pl.pallas_call(pack_kernel, out_shape=[jax.ShapeDtypeStruct(pack, bf16)]...  4.69 us

commit v1 on v0

v1 whole, which is shorter than its diff:
```python
import functools
import math

import jax
import jax.numpy as jnp
from jax import lax
from jax.experimental import pallas as pl
from jax.experimental.pallas import tpu as pltpu
from jax.sharding import PartitionSpec as P

HEAD_SIZE = 128
BLOCK_TOKENS = 128
GROUP = 8
WIDE = 2 * HEAD_SIZE
LAG = 3
LEAD = 2
EDGE_LEAD = 0
DIRECT = 8
CAP = 12
MESH = pl.DeviceIdType.MESH


def pack_kernel(pat, k_ref, v_ref, own_ref, give_ref, sem):
    c = lax.axis_index("ctx")
    entries = pat.shape[2]
    shard_blocks = k_ref.shape[0] // BLOCK_TOKENS

    def each(action, otherwise):
        for n, (row, out_ref) in enumerate(((1 - c, give_ref), (c, own_ref))):
            for p in range(entries):
                at = pat[0, row, p] - c * shard_blocks
                mine = jnp.logical_and(at >= 0, at < shard_blocks)
                here = pl.ds(p * BLOCK_TOKENS, BLOCK_TOKENS)

                @pl.when(mine)
                def _():
                    there = pl.ds(pl.multiple_of(at * BLOCK_TOKENS, BLOCK_TOKENS), BLOCK_TOKENS)
                    for m, ref in enumerate((k_ref, v_ref)):
                        action(pltpu.make_async_copy(ref.at[there, :], out_ref.at[m, here, :], sem.at[n, m, p]))

                if otherwise:
                    @pl.when(jnp.logical_not(mine))
                    def _():
                        zero = jnp.zeros((BLOCK_TOKENS, k_ref.shape[1]), out_ref.dtype)
                        out_ref[0, here, :] = zero
                        out_ref[1, here, :] = zero

    each(lambda copy: copy.start(), True)
    each(lambda copy: copy.wait(), False)


def plain_kernel(q_any, own_any, give_any, att_ref, q_ref, own, recv, kv, in_sem, kv_send, kv_recv):
    peer = 1 - lax.axis_index("ctx")
    take_q = pltpu.make_async_copy(q_any, q_ref, in_sem.at[0])
    take_own = pltpu.make_async_copy(own_any, own, in_sem.at[0])
    take_own.start()
    take_q.start()
    barrier = pltpu.get_barrier_semaphore()
    pl.semaphore_signal(barrier, inc=1, device_id={"ctx": peer}, device_id_type=MESH)
    pl.semaphore_wait(barrier, 1)
    swaps = [remote(give_any.at[n], recv.at[n], kv_send.at[n], kv_recv.at[n], {"ctx": peer}) for n in range(2)]
    for swap in swaps:
        swap.start()
    take_q.wait()
    take_own.wait()
    for n, swap in enumerate(swaps):
        swap.wait()
        kv[n] = own[n] + recv[n]

    def plain(t, carry):
        at = pl.multiple_of(t * WIDE, WIDE)
        lane = pl.ds(pl.multiple_of((t * 2 // GROUP) * HEAD_SIZE, HEAD_SIZE), HEAD_SIZE)
        att_ref[:, pl.ds(at, WIDE)] = two_heads(q_ref[:, pl.ds(at, WIDE)], kv[0, :, lane], kv[1, :, lane])
        return carry

    lax.fori_loop(0, q_ref.shape[1] // WIDE, plain, 0)


def remote(src, dst, send, arrive, where):
    return pltpu.make_async_remote_copy(src_ref=src, dst_ref=dst, send_sem=send, recv_sem=arrive,
                                        device_id=where, device_id_type=MESH)


def two_heads(pair, keys, values):
    tokens = pair.shape[0]
    factor = HEAD_SIZE ** (-0.5) * math.log2(math.e)
    q2 = jnp.concatenate([pair[:, :HEAD_SIZE], pair[:, HEAD_SIZE:]], axis=0)
    scores = lax.dot_general(q2, keys, (((1,), (1,)), ((), ())), preferred_element_type=jnp.float32)
    top = jnp.max(scores, axis=-1, keepdims=True)
    weights = jnp.exp2((scores - top) * factor)
    total = jnp.sum(weights, axis=-1, keepdims=True)
    mixed = jnp.dot(weights.astype(jnp.bfloat16), values, preferred_element_type=jnp.float32)
    out = (mixed / total).astype(jnp.bfloat16)
    return jnp.concatenate([out[:tokens], out[tokens:]], axis=1)


def main_kernel(docs, pat, q_any, k_any, v_any, acc, buf, rows_peer, cols_peer,
                lists, q_ref, give, kv, in_sem, kv_sem, kv_send, kv_recv,
                z_up, z_down, z_recv, x_send, x_more, x_recv, r_send, r_recv, p_send, p_recv, *pieces):
    c = lax.axis_index("ctx")
    h = lax.axis_index("head")
    d = lax.axis_index("doc")
    peer = 1 - c
    tokens, width = q_ref.shape
    chunks = width // WIDE
    half = chunks // 2
    groups = kv.shape[0]
    shard = [pieces[2 * g:2 * g + 2] for g in range(groups)]
    recv = [pieces[2 * (groups + g):2 * (groups + g) + 2] for g in range(groups)]
    shard_blocks = k_any.shape[0]
    entries = pat.shape[2]
    x_next = h + 1 - 2 * (h % 2)
    y_next = (h + 2) % 4

    take_q = pltpu.make_async_copy(q_any, q_ref, in_sem.at[0])

    def take(g, m):
        lane = pl.ds(g * HEAD_SIZE, HEAD_SIZE)
        return pltpu.make_async_copy((k_any, v_any)[m].at[:, :, lane], shard[g][m], kv_sem.at[g, m])

    for g in range(groups):
        for m in range(2):
            take(g, m).start()
        if g == 0:
            take_q.start()

    barrier = pltpu.get_barrier_semaphore()

    def greet(where):
        pl.semaphore_signal(barrier, inc=1, device_id=where, device_id_type=MESH)

    greet({"ctx": peer})
    greet({"head": x_next})
    greet({"head": y_next})

    @pl.when(d > 0)
    def _():
        greet({"doc": d - 1})

    @pl.when(d < docs - 1)
    def _():
        greet({"doc": d + 1})

    for n, row in enumerate((peer, c)):
        count = jnp.int32(0)
        picked = [jnp.int32(0)] * CAP
        for p in range(entries):
            at = pat[0, row, p] - c * shard_blocks
            mine = jnp.logical_and(at >= 0, at < shard_blocks)
            hit = jnp.where(mine, count, -1)
            for s in range(min(p + 1, CAP)):
                picked[s] = jnp.where(hit == s, at, picked[s])
            count = count + jnp.where(mine, 1, 0)
        for s in range(CAP):
            lists[n, s] = picked[s]
        lists[n, CAP] = count

    def block(g, m, n, s):
        return shard[g][m][lists[n, s]]

    def swap(g, m):
        return remote(give.at[g, m], recv[g][m], kv_send.at[g, m], kv_recv.at[g, m], {"ctx": peer})

    def place_of(s):
        return pl.ds(s * BLOCK_TOKENS, BLOCK_TOKENS)

    ends = jnp.where(d > 0, 1, 0) + jnp.where(d < docs - 1, 1, 0)
    for g in range(groups):
        for m in range(2):
            take(g, m).wait()
            for s in range(CAP):
                give[g, m, s] = block(g, m, 0, s)
            if g == 0 and m == 0:
                pl.semaphore_wait(barrier, 3 + ends)
            swap(g, m).start()
    for g in range(groups):
        for m in range(2):
            for s in range(CAP):
                kv[g, m, place_of(s), :] = block(g, m, 1, s)
    take_q.wait()

    def merge(g):
        own = lists[1, CAP]
        for m in range(2):
            swap(g, m).wait_recv()
            for s in range(entries - CAP, entries):
                came = recv[g][m][jnp.clip(s - own, 0, CAP - 1)]
                if s < CAP:
                    came = jnp.where(jnp.full(came.shape, own) > s, kv[g, m, place_of(s), :], came)
                kv[g, m, place_of(s), :] = came

    total_events = docs * chunks
    far = jnp.maximum(d, docs - 1 - d)
    rx = (h % 2 + d % 2) % 2
    ry = (h // 2 + d // 2) % 2
    source = jnp.where(h == d, 0, 1)

    def up(i, k):
        return remote(buf.at[0, i, k], buf.at[0, i, k], z_up.at[i, k], z_recv.at[i, k], {"doc": d + 1})

    def down(i, k):
        return remote(buf.at[0, i, k], buf.at[0, i, k], z_down.at[i, k], z_recv.at[i, k], {"doc": d - 1})

    def row_copy(i, k):
        return remote(buf.at[0, i, k], rows_peer.at[i, k % half], r_send.at[i, k], r_recv.at[i, k], {"ctx": peer})

    def col_copy(i, k):
        return remote(buf.at[source, i, k], cols_peer.at[i, k], p_send.at[i, k], p_recv.at[i, k], {"ctx": peer})

    def plane_copy(i, k, sem, head):
        return remote(buf.at[source, i, k], buf.at[1, i, k], sem.at[i, k], x_recv.at[i, k], {"head": head})

    def place(k):
        even = k % 2 == 0
        return (jnp.where(even, rx, ry), jnp.where(even, ry, rx),
                jnp.where(even, x_next, y_next), jnp.where(even, y_next, x_next))

    def is_direct(s, k):
        return jnp.logical_and(s == far, k >= chunks - DIRECT)

    def item(side, s):
        i = d - s if side == 0 else d + s
        there = (i >= 0) if side == 0 else jnp.logical_and(i < docs, s > 0)
        return i, there

    def z_part(e):
        s, k = e // chunks, e % chunks
        for side in range(2):
            i, there = item(side, s)

            @pl.when(there)
            def _():
                @pl.when(s > 0)
                def _():
                    up(i, k).wait_recv()

                @pl.when(jnp.logical_and(i <= d, d < docs - 1))
                def _():
                    up(i, k).start()

                @pl.when(jnp.logical_and(i >= d, d > 0))
                def _():
                    down(i, k).start()

                @pl.when(k // half != c)
                def _():
                    row_copy(i, k).start()

    def z_ahead(e):
        def bound(e):
            return jnp.clip(e + 1 + lead, chunks, total_events)

        def one(n, carry):
            z_part(n)
            return carry

        lax.fori_loop(bound(e - 1), bound(e), one, 0)

    edge = jnp.logical_or(d == 0, d == docs - 1)
    lead = jnp.where(edge, EDGE_LEAD, LEAD)
    settle = jnp.where(edge, total_events, total_events + LAG)

    def lag(e):
        return jnp.clip(settle - e, 1, LAG)

    def x_part(e):
        for parity in range(2):
            a, b, first, second = place(parity)
            hop = a + b * (3 - 2 * a)

            def one(at, carry):
                s, k = at // chunks, at % chunks
                direct = is_direct(s, k)
                for side in range(2):
                    i, there = item(side, s)

                    @pl.when(there)
                    def _():
                        @pl.when(hop == 0)
                        def _():
                            plane_copy(i, k, x_send, first).start()

                            @pl.when(direct)
                            def _():
                                plane_copy(i, k, x_more, second).start()

                        @pl.when(hop > 0)
                        def _():
                            plane_copy(i, k, x_send, first).wait_recv()

                            @pl.when(hop == 1)
                            def _():
                                plane_copy(i, k, x_send, second).start()

                            @pl.when(jnp.logical_and(hop == 2, jnp.logical_not(direct)))
                            def _():
                                plane_copy(i, k, x_send, first).start()

                        col_copy(i, k).start()

                return carry

            def bound(e):
                return jnp.clip(e + 1 - lag(e) * hop, 0, total_events)

            def half_of(n):
                return (n + 1 - parity) // 2

            lax.fori_loop(half_of(bound(e - 1)), half_of(bound(e)), lambda n, carry: one(2 * n + parity, carry), 0)

    def document(n):
        middle = jnp.where(n == 0, d, jnp.where(n == 1, d - 1, d + 1))
        return jnp.where(d == 0, n, jnp.where(d == docs - 1, d - n, middle))

    def arrived(i):
        def one(k, carry):
            col_copy(i, k).wait_recv()

            @pl.when(k // half == c)
            def _():
                row_copy(i, k).wait_recv()

            return carry

        lax.fori_loop(0, chunks, one, 0)

    def piece(n, carry):
        i, r = document(n // half), n % half

        @pl.when(r == 0)
        def _():
            arrived(i)

        @pl.when(n < half)
        def _():
            add_piece(c, i, r, source, None, acc, buf, rows_peer, cols_peer)

        @pl.when(n >= half)
        def _():
            add_piece(c, i, r, source, acc, acc, buf, rows_peer, cols_peer)

        return carry

    def gram_part(e):
        def done(e):
            first = jnp.clip(e + 1 - chunks - 3 * LAG, 0, half)
            second = jnp.clip(e + 1 - 2 * chunks - 3 * LAG, 0, half)
            third = jnp.where(edge, 2 * jnp.clip(e + 2 - total_events, 0, half // 2),
                              jnp.clip(e + 1 - 2 * chunks - half - 3 * LAG, 0, half))
            return first + second + third

        lax.fori_loop(done(e - 1), done(e), piece, 0)

    def opening(e, carry):
        g = e * 2 // GROUP

        for n in range(groups):
            @pl.when(e == n * GROUP // 2)
            def _():
                merge(n)

        buf[0, d, e] = two_heads(q_ref[:, pl.ds(pl.multiple_of(e * WIDE, WIDE), WIDE)], kv[g, 0], kv[g, 1])
        z_part(e)
        z_ahead(e)
        x_part(e)
        return carry

    def event(e, carry):
        z_ahead(e)
        x_part(e)
        gram_part(e)
        return carry

    lax.fori_loop(0, chunks, opening, 0)
    lax.fori_loop(chunks, total_events + LAG, event, 0)

    for g in range(groups):
        for m in range(2):
            swap(g, m).wait_send()

    def finish(n, carry):
        i, k = n // chunks, n % chunks
        a, b, first, second = place(k)
        hop = a + b * (3 - 2 * a)
        direct = is_direct(jnp.maximum(i - d, d - i), k)

        @pl.when(jnp.logical_and(i <= d, d < docs - 1))
        def _():
            up(i, k).wait_send()

        @pl.when(jnp.logical_and(i >= d, d > 0))
        def _():
            down(i, k).wait_send()

        @pl.when(k // half != c)
        def _():
            row_copy(i, k).wait_send()

        col_copy(i, k).wait_send()

        @pl.when(jnp.logical_or(hop < 2, jnp.logical_and(hop == 2, jnp.logical_not(direct))))
        def _():
            plane_copy(i, k, x_send, first).wait_send()

        @pl.when(jnp.logical_and(hop == 0, direct))
        def _():
            plane_copy(i, k, x_more, second).wait_send()

        return carry

    lax.fori_loop(0, total_events, finish, 0)
    arrived(document(docs - 1) if docs == 2 else jnp.where(d < docs // 2, docs - 1, 0))


def add_piece(c, i, r, source, before, after, buf, rows_peer, cols_peer):
    chunks = cols_peer.shape[1]
    here = pl.ds(pl.multiple_of(r * WIDE, WIDE), WIDE)
    left = jnp.concatenate([buf[0, i, c * (chunks // 2) + r], rows_peer[i, r]], axis=0)
    for k in range(chunks):
        right = jnp.concatenate([buf[source, i, k], cols_peer[i, k]], axis=0)
        lane = pl.ds(k * WIDE, WIDE)
        product = lax.dot_general(left, right, (((0,), (0,)), ((), ())), preferred_element_type=jnp.float32)
        after[here, lane] = product if before is None else before[here, lane] + product


def last_kernel(docs, acc, buf, rows_peer, cols_peer, att_ref, gram_ref, stage, att_sem, gram_sem):
    c = lax.axis_index("ctx")
    h = lax.axis_index("head")
    d = lax.axis_index("doc")
    chunks = cols_peer.shape[1]
    source = jnp.where(h == d, 0, 1)
    i = jnp.where(d < docs // 2, docs - 1, 0)

    def give(r):
        here = pl.ds(r * WIDE, WIDE)
        return pltpu.make_async_copy(stage.at[here, :], gram_ref.at[here, :], gram_sem.at[r])

    def put(k):
        return pltpu.make_async_copy(buf.at[0, d, k], att_ref.at[:, pl.ds(k * WIDE, WIDE)], att_sem.at[k])

    for k in range(chunks):
        put(k).start()
    for r in range(chunks // 2):
        add_piece(c, i, r, source, acc, stage, buf, rows_peer, cols_peer)
        give(r).start()
    for k in range(chunks):
        put(k).wait()
    for r in range(chunks // 2):
        give(r).wait()


def plain(queries, keys, values, pattern):
    tokens, width = queries.shape
    wide = keys.shape[1]
    entries = pattern.shape[2]
    vmem = pl.BlockSpec(memory_space=pltpu.VMEM)
    smem = pl.BlockSpec(memory_space=pltpu.SMEM)
    hbm = pl.BlockSpec(memory_space=pl.ANY)
    pack = (2, entries * BLOCK_TOKENS, wide)
    own, give = pl.pallas_call(
        pack_kernel,
        out_shape=[jax.ShapeDtypeStruct(pack, jnp.bfloat16)] * 2,
        in_specs=[smem, hbm, hbm],
        out_specs=[vmem] * 2,
        scratch_shapes=[pltpu.SemaphoreType.DMA((2, 2, entries))],
    )(pattern, keys, values)
    scratch = [pltpu.VMEM((tokens, width), jnp.bfloat16)] + [pltpu.VMEM(pack, jnp.bfloat16)] * 3
    return pl.pallas_call(
        plain_kernel,
        out_shape=jax.ShapeDtypeStruct((tokens, width), jnp.bfloat16),
        in_specs=[hbm] * 3,
        out_specs=vmem,
        scratch_shapes=scratch + [pltpu.SemaphoreType.DMA((2,))] * 3,
        compiler_params=pltpu.CompilerParams(collective_id=0, has_side_effects=True),
    )(queries, own, give)


def fused(queries, keys, values, pattern, docs):
    tokens, width = queries.shape
    shard_rows, wide = keys.shape
    groups = wide // HEAD_SIZE
    entries = pattern.shape[2]
    chunks = width // WIDE
    bf16, f32 = jnp.bfloat16, jnp.float32
    vmem = pl.BlockSpec(memory_space=pltpu.VMEM)
    hbm = pl.BlockSpec(memory_space=pl.ANY)
    held = [
        pltpu.VMEM((width // 2, width), f32),
        pltpu.VMEM((2, docs, chunks, tokens, WIDE), bf16),
        pltpu.VMEM((docs, chunks // 2, tokens, WIDE), bf16),
        pltpu.VMEM((docs, chunks, tokens, WIDE), bf16),
    ]
    blocks = (shard_rows // BLOCK_TOKENS, BLOCK_TOKENS)
    made = pl.pallas_call(
        functools.partial(main_kernel, docs),
        out_shape=held,
        in_specs=[pl.BlockSpec(memory_space=pltpu.SMEM)] + [hbm] * 3,
        out_specs=[vmem] * 4,
        scratch_shapes=[
            pltpu.SMEM((2, CAP + 1), jnp.int32),
            pltpu.VMEM((tokens, width), bf16),
            pltpu.VMEM((groups, 2, CAP, BLOCK_TOKENS, HEAD_SIZE), bf16),
            pltpu.VMEM((groups, 2, entries * BLOCK_TOKENS, HEAD_SIZE), bf16),
            pltpu.SemaphoreType.DMA((1,)),
        ] + [pltpu.SemaphoreType.DMA((groups, 2))] * 3 + [pltpu.SemaphoreType.DMA((docs, chunks))] * 10
        + [pltpu.VMEM(blocks + (HEAD_SIZE,), bf16)] * (2 * groups)
        + [pltpu.VMEM((CAP, BLOCK_TOKENS, HEAD_SIZE), bf16)] * (2 * groups),
        compiler_params=pltpu.CompilerParams(
            collective_id=0, has_side_effects=True, vmem_limit_bytes=51314688),
    )(pattern, queries, keys.reshape(blocks + (wide,)), values.reshape(blocks + (wide,)))
    return pl.pallas_call(
        functools.partial(last_kernel, docs),
        out_shape=[
            jax.ShapeDtypeStruct((tokens, width), bf16),
            jax.ShapeDtypeStruct((width // 2, width), f32),
        ],
        in_specs=[vmem] * 4,
        out_specs=[hbm] * 2,
        scratch_shapes=[
            pltpu.VMEM((width // 2, width), f32),
            pltpu.SemaphoreType.DMA((chunks,)),
            pltpu.SemaphoreType.DMA((chunks // 2,)),
        ],
        compiler_params=pltpu.CompilerParams(vmem_limit_bytes=32 << 20),
    )(*made)


def per_device(queries, keys, values, pattern):
    ctx_count = lax.axis_size("ctx")
    head_count = lax.axis_size("head")
    doc_count = lax.axis_size("doc")
    owner = lax.axis_index("ctx")
    tok_rows = queries.shape[1]
    width = queries.shape[2]
    direct = head_count == 4 and doc_count == 4
    contract = (((0,), (0,)), ((), ()))
    if direct:
        attended, product = fused(queries[0], keys[0], values[0], pattern, doc_count)
        return (attended[None], product)
    attended = plain(queries[0], keys[0], values[0], pattern)
    sub = width // ctx_count
    model_width = width * head_count
    span = lax.all_gather(attended, "ctx", axis=0, tiled=True)
    mine_cols = lax.dynamic_slice_in_dim(span, owner * sub, sub, 1)
    full_doc = lax.all_gather(span, "head", axis=1, tiled=True)
    slice_width = model_width // doc_count
    split_cols = full_doc.reshape(tok_rows * ctx_count, doc_count, slice_width)
    column_set = lax.all_to_all(split_cols, "doc", split_axis=1, concat_axis=0, tiled=True).reshape(
        doc_count * tok_rows * ctx_count, slice_width)
    product = lax.dot_general(
        lax.all_gather(mine_cols, "doc", axis=0, tiled=True), column_set, contract,
        preferred_element_type=jnp.float32)
    return (attended[None], product)


def solution(mesh):
    placed = (
        P("doc", "ctx", "head"),
        P("doc", "ctx", "head"),
        P("doc", "ctx", "head"),
        P("doc", None, None),
    )
    return jax.shard_map(
        per_device,
        mesh=mesh,
        in_specs=placed,
        out_specs=(P("doc", "ctx", "head"), P(("head", "ctx"), "doc")),
        check_vma=False,
    )
```

time: 74.9 us -> 57.8 us (0.77)
  matrix products: 10.8 us -> 0 us
  Pallas kernels: 62.7 us -> 56.8 us
  local copies, waits for them, and re-layouts: 0.8 us -> 0 us
    dot_general x1 -> x0, matrix products: 10.8 us -> none  [per_device(): lax.dot_general(rows.reshape(tokens, width // ctx_count), cols.reshape(to...]
    pallas_call x2, Pallas kernels: 62.7 us -> 56.8 us  [the longest x1 52.7 us: fused(): pl.pallas_call(functools.partial(main_kernel, docs), out_shape=held, in_s...]
    unnamed x3 -> x0, local copies, waits for them, and re-layouts: 0.8 us -> none
where the time goes in v1:
time: 57.8 us; the launch traced here: 57.4 us
  Pallas kernels  56.8 us (98%)
  between operations  0.64 us (1%)
    pallas_call x1, Pallas kernels, fused(): pl.pallas_call(functools.partial(main_kernel, docs), out_shape=held, in_s...  52.7 us
    pallas_call x1, Pallas kernels, fused(): pl.pallas_call(functools.partial(last_kernel, docs), out_shape=[jax.Shape...  4.02 us

profile of v1, /device:TPU:25, one launch (start us, length us, event | category | flops | bytes accessed | tf_op | source)
XLA Modules:
  0.0 57.4 jit_solution(5981138790756949708)
XLA Ops:
  0.6 52.7 %shard_map.59 = (f32[1024,2048]{1,0:T(8,128)S(1)}, bf16[2,4,8,128,256]{4,3,2,1,0:T(8,128)(2,1)S(1)}, bf16[4,4,128,256]{3,2,1,0:T(8,128)(2,1)S(1)}, bf16[4,8,128,256]{3,2,1,0:T(8,128)(2,1)S(1)}) custom-call(s32[1,2,16]{2,1,0:T(2,128)} %pat.1, bf16[128,2048]{1,0:T(8,128)(2,1)} %bitcast.6, bf16[32,128,256]{2,1,0:T(8,128)(2,1)} %bitcast.4, ...), custom_call_target="tpu_custom_call" | custom-call | tf_op jit(solution)/shard_map/pallas_call | solution.py:494
  53.4 4.0 %shard_map.60 = (bf16[128,2048]{1,0:T(8,128)(2,1)}, f32[1024,2048]{1,0:T(8,128)}) custom-call(f32[1024,2048]{1,0:T(8,128)S(1)} %get-tuple-element.8.acc, bf16[2,4,8,128,256]{4,3,2,1,0:T(8,128)(2,1)S(1)} %get-tuple-element.9.buf, bf16[4,4,128,256]{3,2,1,0:T(8,128)(2,1)S(1)} %get-tuple-element.10.rows_peer, ...), custom_call_target="tpu_custom_call" | custom-call | tf_op jit(solution)/shard_map/pallas_call | solution.py:511

commit v2 on v1

--- a/solution.py
+++ b/solution.py
@@ -17,6 +17,8 @@
 EDGE_LEAD = 0
 DIRECT = 8
 CAP = 12
+SPENT = 11
+PARTS = 1
 MESH = pl.DeviceIdType.MESH
 
 
@@ -195,11 +197,16 @@
     ry = (h // 2 + d // 2) % 2
     source = jnp.where(h == d, 0, 1)
 
-    def up(i, k):
-        return remote(buf.at[0, i, k], buf.at[0, i, k], z_up.at[i, k], z_recv.at[i, k], {"doc": d + 1})
-
-    def down(i, k):
-        return remote(buf.at[0, i, k], buf.at[0, i, k], z_down.at[i, k], z_recv.at[i, k], {"doc": d - 1})
+    def part_of(p):
+        return pl.ds(p * (tokens // PARTS), tokens // PARTS)
+
+    def up(i, k, p):
+        ref = buf.at[0, i, k, part_of(p)]
+        return remote(ref, ref, z_up.at[i, k, p], z_recv.at[i, k, p], {"doc": d + 1})
+
+    def down(i, k, p):
+        ref = buf.at[0, i, k, part_of(p)]
+        return remote(ref, ref, z_down.at[i, k, p], z_recv.at[i, k, p], {"doc": d - 1})
 
     def row_copy(i, k):
         return remote(buf.at[0, i, k], rows_peer.at[i, k % half], r_send.at[i, k], r_recv.at[i, k], {"ctx": peer})
@@ -207,8 +214,9 @@
     def col_copy(i, k):
         return remote(buf.at[source, i, k], cols_peer.at[i, k], p_send.at[i, k], p_recv.at[i, k], {"ctx": peer})
 
-    def plane_copy(i, k, sem, head):
-        return remote(buf.at[source, i, k], buf.at[1, i, k], sem.at[i, k], x_recv.at[i, k], {"head": head})
+    def plane_copy(i, k, p, sem, head):
+        return remote(buf.at[source, i, k, part_of(p)], buf.at[1, i, k, part_of(p)], sem.at[i, k, p],
+                      x_recv.at[i, k, p], {"head": head})
 
     def place(k):
         even = k % 2 == 0
@@ -230,17 +238,18 @@
 
             @pl.when(there)
             def _():
-                @pl.when(s > 0)
-                def _():
-                    up(i, k).wait_recv()
-
-                @pl.when(jnp.logical_and(i <= d, d < docs - 1))
-                def _():
-                    up(i, k).start()
-
-                @pl.when(jnp.logical_and(i >= d, d > 0))
-                def _():
-                    down(i, k).start()
+                for p in range(PARTS):
+                    @pl.when(s > 0)
+                    def _():
+                        up(i, k, p).wait_recv()
+
+                    @pl.when(jnp.logical_and(i <= d, d < docs - 1))
+                    def _():
+                        up(i, k, p).start()
+
+                    @pl.when(jnp.logical_and(i >= d, d > 0))
+                    def _():
+                        down(i, k, p).start()
 
                 @pl.when(k // half != c)
                 def _():
@@ -276,25 +285,26 @@
 
                     @pl.when(there)
                     def _():
-                        @pl.when(hop == 0)
-                        def _():
-                            plane_copy(i, k, x_send, first).start()
-
-                            @pl.when(direct)
+                        for p in range(PARTS):
+                            @pl.when(hop == 0)
                             def _():
-                                plane_copy(i, k, x_more, second).start()
-
-                        @pl.when(hop > 0)
-                        def _():
-                            plane_copy(i, k, x_send, first).wait_recv()
-
-                            @pl.when(hop == 1)
+                                plane_copy(i, k, p, x_send, first).start()
+
+                                @pl.when(direct)
+                                def _():
+                                    plane_copy(i, k, p, x_more, second).start()
+
+                            @pl.when(hop > 0)
                             def _():
-                                plane_copy(i, k, x_send, second).start()
-
-                            @pl.when(jnp.logical_and(hop == 2, jnp.logical_not(direct)))
-                            def _():
-                                plane_copy(i, k, x_send, first).start()
+                                plane_copy(i, k, p, x_send, first).wait_recv()
+
+                                @pl.when(hop == 1)
+                                def _():
+                                    plane_copy(i, k, p, x_send, second).start()
+
+                                @pl.when(jnp.logical_and(hop == 2, jnp.logical_not(direct)))
+                                def _():
+                                    plane_copy(i, k, p, x_send, first).start()
 
                         col_copy(i, k).start()
 
@@ -351,6 +361,41 @@
 
         lax.fori_loop(done(e - 1), done(e), piece, 0)
 
+    def finish(e, carry):
+        s, k = e // chunks, e % chunks
+        a, b, first, second = place(k)
+        hop = a + b * (3 - 2 * a)
+        direct = is_direct(s, k)
+        for side in range(2):
+            i, there = item(side, s)
+
+            @pl.when(there)
+            def _():
+                for p in range(PARTS):
+                    @pl.when(jnp.logical_and(i <= d, d < docs - 1))
+                    def _():
+                        up(i, k, p).wait_send()
+
+                    @pl.when(jnp.logical_and(i >= d, d > 0))
+                    def _():
+                        down(i, k, p).wait_send()
+
+                    @pl.when(jnp.logical_or(hop < 2, jnp.logical_and(hop == 2, jnp.logical_not(direct))))
+                    def _():
+                        plane_copy(i, k, p, x_send, first).wait_send()
+
+                    @pl.when(jnp.logical_and(hop == 0, direct))
+                    def _():
+                        plane_copy(i, k, p, x_more, second).wait_send()
+
+                @pl.when(k // half != c)
+                def _():
+                    row_copy(i, k).wait_send()
+
+                col_copy(i, k).wait_send()
+
+        return carry
+
     def opening(e, carry):
         g = e * 2 // GROUP
 
@@ -369,46 +414,19 @@
         z_ahead(e)
         x_part(e)
         gram_part(e)
+
+        @pl.when(e >= SPENT)
+        def _():
+            finish(e - SPENT, 0)
+
         return carry
 
     lax.fori_loop(0, chunks, opening, 0)
-    lax.fori_loop(chunks, total_events + LAG, event, 0)
-
     for g in range(groups):
         for m in range(2):
             swap(g, m).wait_send()
-
-    def finish(n, carry):
-        i, k = n // chunks, n % chunks
-        a, b, first, second = place(k)
-        hop = a + b * (3 - 2 * a)
-        direct = is_direct(jnp.maximum(i - d, d - i), k)
-
-        @pl.when(jnp.logical_and(i <= d, d < docs - 1))
-        def _():
-            up(i, k).wait_send()
-
-        @pl.when(jnp.logical_and(i >= d, d > 0))
-        def _():
-            down(i, k).wait_send()
-
-        @pl.when(k // half != c)
-        def _():
-            row_copy(i, k).wait_send()
-
-        col_copy(i, k).wait_send()
-
-        @pl.when(jnp.logical_or(hop < 2, jnp.logical_and(hop == 2, jnp.logical_not(direct))))
-        def _():
-            plane_copy(i, k, x_send, first).wait_send()
-
-        @pl.when(jnp.logical_and(hop == 0, direct))
-        def _():
-            plane_copy(i, k, x_more, second).wait_send()
-
-        return carry
-
-    lax.fori_loop(0, total_events, finish, 0)
+    lax.fori_loop(chunks, total_events + LAG, event, 0)
+    lax.fori_loop(total_events + LAG - SPENT, total_events, finish, 0)
     arrived(document(docs - 1) if docs == 2 else jnp.where(d < docs // 2, docs - 1, 0))
 
 
@@ -502,7 +520,8 @@
             pltpu.VMEM((groups, 2, CAP, BLOCK_TOKENS, HEAD_SIZE), bf16),
             pltpu.VMEM((groups, 2, entries * BLOCK_TOKENS, HEAD_SIZE), bf16),
             pltpu.SemaphoreType.DMA((1,)),
-        ] + [pltpu.SemaphoreType.DMA((groups, 2))] * 3 + [pltpu.SemaphoreType.DMA((docs, chunks))] * 10
+        ] + [pltpu.SemaphoreType.DMA((groups, 2))] * 3 + [pltpu.SemaphoreType.DMA((docs, chunks, PARTS))] * 6
+        + [pltpu.SemaphoreType.DMA((docs, chunks))] * 4
         + [pltpu.VMEM(blocks + (HEAD_SIZE,), bf16)] * (2 * groups)
         + [pltpu.VMEM((CAP, BLOCK_TOKENS, HEAD_SIZE), bf16)] * (2 * groups),
         compiler_params=pltpu.CompilerParams(

time: 57.8 us -> 57.6 us (level)
  no operation moved by 1% of the time
where the time goes in v2:
time: 57.6 us; the launch traced here: 57.4 us
  Pallas kernels  56.8 us (99%)
  between operations  0.64 us (1%)
    pallas_call x1, Pallas kernels, fused(): pl.pallas_call(functools.partial(main_kernel, docs), out_shape=held, in_s...  52.7 us
    pallas_call x1, Pallas kernels, fused(): pl.pallas_call(functools.partial(last_kernel, docs), out_shape=[jax.Shape...  4.02 us

profile of v2, /device:TPU:25, one launch (start us, length us, event | category | flops | bytes accessed | tf_op | source)
XLA Modules:
  0.0 57.4 jit_solution(5281222983609044572)
XLA Ops:
  0.6 52.7 %shard_map.59 = (f32[1024,2048]{1,0:T(8,128)S(1)}, bf16[2,4,8,128,256]{4,3,2,1,0:T(8,128)(2,1)S(1)}, bf16[4,4,128,256]{3,2,1,0:T(8,128)(2,1)S(1)}, bf16[4,8,128,256]{3,2,1,0:T(8,128)(2,1)S(1)}) custom-call(s32[1,2,16]{2,1,0:T(2,128)} %pat.1, bf16[128,2048]{1,0:T(8,128)(2,1)} %bitcast.6, bf16[32,128,256]{2,1,0:T(8,128)(2,1)} %bitcast.4, ...), custom_call_target="tpu_custom_call" | custom-call | tf_op jit(solution)/shard_map/pallas_call | solution.py:512
  53.4 4.0 %shard_map.60 = (bf16[128,2048]{1,0:T(8,128)(2,1)}, f32[1024,2048]{1,0:T(8,128)}) custom-call(f32[1024,2048]{1,0:T(8,128)S(1)} %get-tuple-element.8.acc, bf16[2,4,8,128,256]{4,3,2,1,0:T(8,128)(2,1)S(1)} %get-tuple-element.9.buf, bf16[4,4,128,256]{3,2,1,0:T(8,128)(2,1)S(1)} %get-tuple-element.10.rows_peer, ...), custom_call_target="tpu_custom_call" | custom-call | tf_op jit(solution)/shard_map/pallas_call | solution.py:530
